TPU v7x, 32 devices: a whole 2x2x4 slice. The times are simulated.
32 devices in a mesh: dp: 8 (over z, y), fsdp: 4 (over x, core).
Axes of the slice: x: 2, y: 2, z: 4, core: 2. Of those that a mesh axis runs over, the one named last changes fastest.
Arguments:
- hidden_in: bfloat16 [2, 32, 256, 768], P(None, ('dp', 'fsdp')), may hold values from -6 to 6
- patches: bfloat16 [2, 32, 2048, 768], P(None, ('dp', 'fsdp')), may hold values from -6 to 6
- token_segments: int32 [2, 32, 256], P(None, ('dp', 'fsdp')), may hold values from 0 to 3, as said below
- patch_segments: int32 [2, 32, 2048], P(None, ('dp', 'fsdp')), may hold values from 0 to 3, as said below
- cotangent: bfloat16 [2, 32, 256, 768], P(None, ('dp', 'fsdp')), may hold values from -6 to 6
- attention_weights: float32 [8, 768, 768], P(None, 'fsdp', 'dp'), may hold values from -1.1547005 to 1.1547005
- attention_means: float32 [8, 768, 768], P(None, 'fsdp', 'dp'), may hold values from -40 to 40
- attention_squares: float32 [8, 768, 768], P(None, 'fsdp', 'dp'), may hold values from 131.072 to 1638.4
- inner_weights: float32 [2, 768, 2048], P(None, 'fsdp', 'dp'), may hold values from -0.21875 to 0.21875
- inner_means: float32 [2, 768, 2048], P(None, 'fsdp', 'dp'), may hold values from -40 to 40
- inner_squares: float32 [2, 768, 2048], P(None, 'fsdp', 'dp'), may hold values from 131.072 to 1638.4
- outer_weights: float32 [2048, 768], P('fsdp', 'dp'), may hold values from -0.125 to 0.125
- outer_means: float32 [2048, 768], P('fsdp', 'dp'), may hold values from -48 to 48
- outer_squares: float32 [2048, 768], P('fsdp', 'dp'), may hold values from 163.84 to 2457.6
- norm_gains: float32 [3, 768], P(None, 'fsdp'), may hold values from 0.25 to 1.75
- gain_means: float32 [3, 768], P(None, 'fsdp'), may hold values from -80 to 80
- gain_squares: float32 [3, 768], P(None, 'fsdp'), may hold values from 425.984 to 6881.28
Outputs:
- hidden_out: bfloat16 [2, 32, 256, 768], P(None, ('dp', 'fsdp'))
- hidden_grad: float32 [2, 32, 256, 768], P(None, ('dp', 'fsdp'))
- patch_grad: float32 [2, 32, 2048, 768], P(None, ('dp', 'fsdp'))
- attention_mean: float32 [8, 768, 768], P(None, 'fsdp', 'dp')
- attention_square: float32 [8, 768, 768], P(None, 'fsdp', 'dp')
- attention_master: float32 [8, 768, 768], P(None, 'fsdp', 'dp')
- attention_copy: bfloat16 [8, 768, 768], P(None, 'fsdp', 'dp')
- inner_mean: float32 [2, 768, 2048], P(None, 'fsdp', 'dp')
- inner_square: float32 [2, 768, 2048], P(None, 'fsdp', 'dp')
- inner_master: float32 [2, 768, 2048], P(None, 'fsdp', 'dp')
- inner_copy: bfloat16 [2, 768, 2048], P(None, 'fsdp', 'dp')
- outer_mean: float32 [2048, 768], P('fsdp', 'dp')
- outer_square: float32 [2048, 768], P('fsdp', 'dp')
- outer_master: float32 [2048, 768], P('fsdp', 'dp')
- outer_copy: bfloat16 [2048, 768], P('fsdp', 'dp')
- gain_mean: float32 [3, 768], P(None, 'fsdp')
- gain_square: float32 [3, 768], P(None, 'fsdp')
- gain_master: float32 [3, 768], P(None, 'fsdp')
- gain_copy: bfloat16 [3, 768], P(None, 'fsdp')
Inputs may be any that keep to these rules, and one draw needn't show every extreme that they name: `token_segments`: along each row the ids never fall from one token to the next, and each of the 4 ids holds one token or more. `patch_segments`: along each row the ids never fall from one patch to the next, and each of the 4 ids holds one patch or more.
All inputs are finite; a program needn't handle non-finite values.
Results may differ from a plain program's by a relative error of at most 0.02.
The roundings to bfloat16 on the way count: a program that leaves them out, or rounds other values in their place, can miss the bound.
Values may be sent and summed in bfloat16 or wider, within the bound.
A program may use at most 320 MiB of HBM per device.

v0:
```python
import jax
import jax.numpy as jnp
from jax import lax
from jax.sharding import PartitionSpec as P

D = 768
HEADS = 12
HEAD = 64
STEP = 10
epsilon = 1e-06
score_scale = 0.125
masked_value = -1000000000.0
beta_one = 0.9
beta_two = 0.95
adam_epsilon = 1e-08
decay_matrix = 0.1
rate_matrix = 0.1
rate_gain = 0.3
float_type = jnp.float32
brain_type = jnp.bfloat16


def gelu_tanh(values):
    return (
        0.5
        * values
        * (1.0 + jnp.tanh(0.7978845608028654 * (values + 0.044715 * values * values * values)))
    )


def split_heads(matrix):
    return matrix.reshape(matrix.shape[:-1] + (HEADS, HEAD))


def norm_forward(values, gain):
    inverse_rms = lax.rsqrt(jnp.mean(values * values, axis=-1, keepdims=True) + epsilon)
    unit_rows = values * inverse_rms
    return (unit_rows * gain.astype(float_type), unit_rows, inverse_rms)


def norm_backward(grad_rows, gain, unit_rows, inverse_rms):
    grad_unit = grad_rows * gain.astype(float_type)
    grad_values = inverse_rms * (
        grad_unit - unit_rows * jnp.mean(grad_unit * unit_rows, axis=-1, keepdims=True)
    )
    return (grad_values, jnp.sum(grad_rows * unit_rows, axis=0))


def softmax_rows(scores):
    row_maximum = jnp.max(scores, axis=-1, keepdims=True)
    raised = jnp.exp(scores - row_maximum)
    return raised / jnp.sum(raised, axis=-1, keepdims=True)


def attend_forward(queries, key_heads, value_heads, allowed):
    scores = score_scale * jnp.einsum(
        "qhe,khe->hqk", queries, key_heads, preferred_element_type=float_type
    )
    probabilities = softmax_rows(jnp.where(allowed[None], scores, masked_value))
    rounded_probs = probabilities.astype(brain_type)
    mixture = jnp.einsum(
        "hqk,khe->qhe", rounded_probs, value_heads, preferred_element_type=float_type
    )
    return (mixture.astype(brain_type), probabilities, rounded_probs)


def attend_backward(grad_mixture, queries, key_heads, value_heads, probabilities, rounded_probs):
    grad_probs = jnp.einsum(
        "qhe,khe->hqk", grad_mixture, value_heads, preferred_element_type=float_type
    )
    grad_values = jnp.einsum(
        "hqk,qhe->khe", rounded_probs, grad_mixture, preferred_element_type=float_type
    ).astype(brain_type)
    row_inner = jnp.sum(probabilities * grad_probs, axis=-1, keepdims=True)
    grad_scores = (probabilities * (grad_probs - row_inner)).astype(brain_type)
    grad_queries = (
        score_scale
        * jnp.einsum("hqk,khe->qhe", grad_scores, key_heads, preferred_element_type=float_type)
    ).astype(brain_type)
    grad_keys = (
        score_scale
        * jnp.einsum("hqk,qhe->khe", grad_scores, queries, preferred_element_type=float_type)
    ).astype(brain_type)
    return (grad_queries, grad_keys, grad_values)


def layer_forward(weights, hidden, patch_rows, token_ids, patch_ids):
    attention, inner_matrix, outer_matrix, gain_rows = weights
    length = hidden.shape[0]
    initial = hidden.astype(float_type)
    normed_one, unit_one, rms_one = norm_forward(initial, gain_rows[0])
    normed_one = normed_one.astype(brain_type)
    projected = jnp.einsum(
        "nd,kde->kne", normed_one, attention[0:3], preferred_element_type=float_type
    ).astype(brain_type)
    heads_in = split_heads(projected)
    places = jnp.arange(length)
    causal = (places[:, None] >= places[None, :]) & (token_ids[:, None] == token_ids[None, :])
    mixture_one, probs_one, rounded_one = attend_forward(
        heads_in[0], heads_in[1], heads_in[2], causal
    )
    mixture_one = mixture_one.reshape(length, D)
    after_one = initial + jnp.dot(mixture_one, attention[3], preferred_element_type=float_type)
    normed_two, unit_two, rms_two = norm_forward(after_one, gain_rows[1])
    normed_two = normed_two.astype(brain_type)
    cross_query = split_heads(
        jnp.dot(normed_two, attention[4], preferred_element_type=float_type).astype(brain_type)
    )
    cross_pair = split_heads(
        jnp.einsum(
            "pd,kde->kpe", patch_rows, attention[5:7], preferred_element_type=float_type
        ).astype(brain_type)
    )
    matching = token_ids[:, None] == patch_ids[None, :]
    mixture_two, probs_two, rounded_two = attend_forward(
        cross_query, cross_pair[0], cross_pair[1], matching
    )
    mixture_two = mixture_two.reshape(length, D)
    after_two = after_one + jnp.dot(mixture_two, attention[7], preferred_element_type=float_type)
    normed_three, unit_three, rms_three = norm_forward(after_two, gain_rows[2])
    normed_three = normed_three.astype(brain_type)
    gated = jnp.einsum("nd,kdf->knf", normed_three, inner_matrix, preferred_element_type=float_type)
    units = (gelu_tanh(gated[0]) * gated[1]).astype(brain_type)
    layer_out = (
        after_two + jnp.dot(units, outer_matrix, preferred_element_type=float_type)
    ).astype(brain_type)
    stored = {
        "unit_one": unit_one,
        "rms_one": rms_one,
        "normed_one": normed_one,
        "heads_in": heads_in,
        "probs_one": probs_one,
        "rounded_one": rounded_one,
        "mixture_one": mixture_one,
        "unit_two": unit_two,
        "rms_two": rms_two,
        "normed_two": normed_two,
        "cross_query": cross_query,
        "cross_pair": cross_pair,
        "probs_two": probs_two,
        "rounded_two": rounded_two,
        "mixture_two": mixture_two,
        "unit_three": unit_three,
        "rms_three": rms_three,
        "normed_three": normed_three,
        "gated": gated,
        "units": units,
    }
    return (layer_out, stored)


def layer_backward(weights, stored, cotangent_row, patch_rows):
    attention, inner_matrix, outer_matrix, gain_rows = weights
    length = cotangent_row.shape[0]
    grad_final = cotangent_row.astype(float_type)
    grad_low = grad_final.astype(brain_type)
    grad_outer = jnp.einsum(
        "nf,nd->fd", stored["units"], grad_low, preferred_element_type=float_type
    )
    grad_units = jnp.einsum("nd,fd->nf", grad_low, outer_matrix, preferred_element_type=float_type)
    gate_in = stored["gated"][0]
    up_in = stored["gated"][1]
    activation, gelu_back = jax.vjp(gelu_tanh, gate_in)
    grad_gate = gelu_back(grad_units * up_in)[0]
    grad_gated = jnp.stack([grad_gate, grad_units * activation]).astype(brain_type)
    grad_inner = jnp.einsum(
        "nd,knf->kdf", stored["normed_three"], grad_gated, preferred_element_type=float_type
    )
    grad_normed = jnp.einsum(
        "knf,kdf->nd", grad_gated, inner_matrix, preferred_element_type=float_type
    )
    grad_from_three, gain_three = norm_backward(
        grad_normed, gain_rows[2], stored["unit_three"], stored["rms_three"]
    )
    grad_after_two = grad_final + grad_from_three
    branch_two = grad_after_two.astype(brain_type)
    grad_cross_out = jnp.einsum(
        "nd,ne->de", stored["mixture_two"], branch_two, preferred_element_type=float_type
    )
    grad_mixture_two = split_heads(
        jnp.einsum("ne,de->nd", branch_two, attention[7], preferred_element_type=float_type).astype(
            brain_type
        )
    )
    cross_pair = stored["cross_pair"]
    grad_cq, grad_ck, grad_cv = attend_backward(
        grad_mixture_two,
        stored["cross_query"],
        cross_pair[0],
        cross_pair[1],
        stored["probs_two"],
        stored["rounded_two"],
    )
    grad_cq = grad_cq.reshape(length, D)
    grad_pair = jnp.stack([grad_ck, grad_cv]).reshape(2, patch_rows.shape[0], D)
    grad_cross_query = jnp.einsum(
        "nd,ne->de", stored["normed_two"], grad_cq, preferred_element_type=float_type
    )
    grad_cross_pair = jnp.einsum(
        "pd,kpe->kde", patch_rows, grad_pair, preferred_element_type=float_type
    )
    patch_grad = jnp.einsum(
        "kpe,kde->pd", grad_pair, attention[5:7], preferred_element_type=float_type
    )
    grad_normed_two = jnp.einsum(
        "ne,de->nd", grad_cq, attention[4], preferred_element_type=float_type
    )
    grad_from_two, gain_two = norm_backward(
        grad_normed_two, gain_rows[1], stored["unit_two"], stored["rms_two"]
    )
    grad_after_one = grad_after_two + grad_from_two
    branch_one = grad_after_one.astype(brain_type)
    grad_self_out = jnp.einsum(
        "nd,ne->de", stored["mixture_one"], branch_one, preferred_element_type=float_type
    )
    grad_mixture_one = split_heads(
        jnp.einsum("ne,de->nd", branch_one, attention[3], preferred_element_type=float_type).astype(
            brain_type
        )
    )
    heads_in = stored["heads_in"]
    grad_query, grad_key, grad_value = attend_backward(
        grad_mixture_one,
        heads_in[0],
        heads_in[1],
        heads_in[2],
        stored["probs_one"],
        stored["rounded_one"],
    )
    grad_projected = jnp.stack([grad_query, grad_key, grad_value]).reshape(3, length, D)
    grad_self_in = jnp.einsum(
        "nd,kne->kde", stored["normed_one"], grad_projected, preferred_element_type=float_type
    )
    grad_normed_one = jnp.einsum(
        "kne,kde->nd", grad_projected, attention[0:3], preferred_element_type=float_type
    )
    grad_from_one, gain_one = norm_backward(
        grad_normed_one, gain_rows[0], stored["unit_one"], stored["rms_one"]
    )
    hidden_grad = grad_after_one + grad_from_one
    grad_attention = jnp.concatenate(
        [
            grad_self_in,
            grad_self_out[None],
            grad_cross_query[None],
            grad_cross_pair,
            grad_cross_out[None],
        ],
        axis=0,
    )
    grad_gains = jnp.stack([gain_one, gain_two, gain_three])
    return (hidden_grad, patch_grad, (grad_attention, grad_inner, grad_outer, grad_gains))


def fetch_forward(copies):
    widened = (
        lax.all_gather(copies[0], "fsdp", axis=1, tiled=True),
        lax.all_gather(copies[1], "fsdp", axis=1, tiled=True),
        lax.all_gather(copies[2], "fsdp", axis=0, tiled=True),
        lax.all_gather(copies[3], "fsdp", axis=1, tiled=True),
    )
    complete = (
        lax.all_gather(widened[0], "dp", axis=2, tiled=True),
        lax.all_gather(widened[1], "dp", axis=2, tiled=True),
        lax.all_gather(widened[2], "dp", axis=1, tiled=True),
    )
    return (complete[0], complete[1], complete[2], widened[3])


def fetch_backward(copies):
    widened = (
        lax.all_gather(copies[0], "fsdp", axis=1, tiled=True),
        lax.all_gather(copies[1], "fsdp", axis=1, tiled=True),
        lax.all_gather(copies[2], "fsdp", axis=0, tiled=True),
        lax.all_gather(copies[3], "fsdp", axis=1, tiled=True),
    )
    complete = (
        lax.all_gather(widened[0], "dp", axis=2, tiled=True),
        lax.all_gather(widened[1], "dp", axis=2, tiled=True),
        lax.all_gather(widened[2], "dp", axis=1, tiled=True),
    )
    return (complete[0], complete[1], complete[2], widened[3])


def reduce_grads(totals):
    partial_sums = (
        lax.psum_scatter(totals[0], "dp", scatter_dimension=2, tiled=True),
        lax.psum_scatter(totals[1], "dp", scatter_dimension=2, tiled=True),
        lax.psum_scatter(totals[2], "dp", scatter_dimension=1, tiled=True),
    )
    gain_totals = lax.psum(totals[3], "dp")
    return (
        lax.psum_scatter(partial_sums[0], "fsdp", scatter_dimension=1, tiled=True),
        lax.psum_scatter(partial_sums[1], "fsdp", scatter_dimension=1, tiled=True),
        lax.psum_scatter(partial_sums[2], "fsdp", scatter_dimension=0, tiled=True),
        lax.psum_scatter(gain_totals, "fsdp", scatter_dimension=1, tiled=True),
    )


def adam_update(weight, mean_old, square_old, gradient, step_rate, decay_rate):
    mean_new = beta_one * mean_old + (1.0 - beta_one) * gradient
    square_new = beta_two * square_old + (1.0 - beta_two) * gradient * gradient
    corrected = (
        mean_new
        / (1.0 - beta_one**STEP)
        / (jnp.sqrt(square_new / (1.0 - beta_two**STEP)) + adam_epsilon)
    )
    master = weight - step_rate * (corrected + decay_rate * weight)
    return (mean_new, square_new, master, master.astype(jnp.bfloat16))


def on_device(
    hidden_in,
    patches,
    token_segments,
    patch_segments,
    cotangent,
    attention_weights,
    attention_means,
    attention_squares,
    inner_weights,
    inner_means,
    inner_squares,
    outer_weights,
    outer_means,
    outer_squares,
    norm_gains,
    gain_means,
    gain_squares,
):
    copies = (
        attention_weights.astype(brain_type),
        inner_weights.astype(brain_type),
        outer_weights.astype(brain_type),
        norm_gains.astype(brain_type),
    )
    layer_outputs = []
    input_grads = []
    patch_grads = []
    totals = None
    for batch_index in range(hidden_in.shape[0]):
        forward_weights = fetch_forward(copies)
        layer_out, stored = layer_forward(
            forward_weights,
            hidden_in[batch_index, 0],
            patches[batch_index, 0],
            token_segments[batch_index, 0],
            patch_segments[batch_index, 0],
        )
        backward_weights = fetch_backward(copies)
        hidden_grad, patch_grad, gradients = layer_backward(
            backward_weights, stored, cotangent[batch_index, 0], patches[batch_index, 0]
        )
        layer_outputs.append(layer_out)
        input_grads.append(hidden_grad)
        patch_grads.append(patch_grad)
        totals = gradients if totals is None else jax.tree.map(jnp.add, totals, gradients)
    owned_grads = reduce_grads(totals)
    attention_new = adam_update(
        attention_weights,
        attention_means,
        attention_squares,
        owned_grads[0],
        rate_matrix,
        decay_matrix,
    )
    inner_new = adam_update(
        inner_weights, inner_means, inner_squares, owned_grads[1], rate_matrix, decay_matrix
    )
    outer_new = adam_update(
        outer_weights, outer_means, outer_squares, owned_grads[2], rate_matrix, decay_matrix
    )
    gain_new = adam_update(norm_gains, gain_means, gain_squares, owned_grads[3], rate_gain, 0.0)
    hidden_out = jnp.stack(layer_outputs)[:, None]
    hidden_grads = jnp.stack(input_grads)[:, None]
    patch_grads_all = jnp.stack(patch_grads)[:, None]
    return (
        hidden_out,
        hidden_grads,
        patch_grads_all,
        attention_new[0],
        attention_new[1],
        attention_new[2],
        attention_new[3],
        inner_new[0],
        inner_new[1],
        inner_new[2],
        inner_new[3],
        outer_new[0],
        outer_new[1],
        outer_new[2],
        outer_new[3],
        gain_new[0],
        gain_new[1],
        gain_new[2],
        gain_new[3],
    )


def solution(mesh):
    placed = (
        P(None, ("dp", "fsdp"), None, None),
        P(None, ("dp", "fsdp"), None, None),
        P(None, ("dp", "fsdp"), None),
        P(None, ("dp", "fsdp"), None),
        P(None, ("dp", "fsdp"), None, None),
        P(None, "fsdp", "dp"),
        P(None, "fsdp", "dp"),
        P(None, "fsdp", "dp"),
        P(None, "fsdp", "dp"),
        P(None, "fsdp", "dp"),
        P(None, "fsdp", "dp"),
        P("fsdp", "dp"),
        P("fsdp", "dp"),
        P("fsdp", "dp"),
        P(None, "fsdp"),
        P(None, "fsdp"),
        P(None, "fsdp"),
    )
    return jax.shard_map(
        on_device,
        mesh=mesh,
        in_specs=placed,
        out_specs=(
            P(None, ("dp", "fsdp"), None, None),
            P(None, ("dp", "fsdp"), None, None),
            P(None, ("dp", "fsdp"), None, None),
            P(None, "fsdp", "dp"),
            P(None, "fsdp", "dp"),
            P(None, "fsdp", "dp"),
            P(None, "fsdp", "dp"),
            P(None, "fsdp", "dp"),
            P(None, "fsdp", "dp"),
            P(None, "fsdp", "dp"),
            P(None, "fsdp", "dp"),
            P("fsdp", "dp"),
            P("fsdp", "dp"),
            P("fsdp", "dp"),
            P("fsdp", "dp"),
            P(None, "fsdp"),
            P(None, "fsdp"),
            P(None, "fsdp"),
            P(None, "fsdp"),
        ),
        check_vma=False,
    )
```

profile of v0, /device:TPU:0, one launch (start us, length us, event | category | flops | bytes accessed | tf_op | source)
XLA Modules:
  0.0 1277.1 jit_solution(9727439426056397318)
XLA Ops:
  9.8 22.8 %all-gather.6.cloned.1.call-done = bf16[8,768,96]{2,0,1:T(8,128)(2,1)} async-done(((bf16[8,192,96]{2,0,1:T(8,128)(2,1)}), bf16[8,768,96]{2,0,1:T(8,128)(2,1)}) %all-gather.6.cloned.1.call-update) | async-done | bytes 1179664 | tf_op jit(solution)/shard_map/all_gather | solution.py:257
  35.8 9.0 all_gather.17
  54.9 118.2 %all-gather.8.cloned.1.call-done = bf16[8,768,768]{1,0,2:T(8,128)(2,1)} async-done(((bf16[8,768,96]{1,0,2:T(8,128)(2,1)}), bf16[8,768,768]{1,0,2:T(8,128)(2,1)}) %all-gather.8.cloned.1.call-update) | async-done | bytes 9437200 | tf_op jit(solution)/shard_map/all_gather | solution.py:263
  173.2 7.1 slice.179
  180.2 8.3 copy.479
  188.5 18.3 %fusion.261 = (bf16[1,768,768]{1,0,2:T(2,128)(2,1)}, bf16[1,768,768]{1,0,2:T(2,128)(2,1)}, bf16[1,768,768]{1,0,2:T(2,128)(2,1)}) fusion(bf16[8,768,768]{1,0,2:T(8,128)(2,1)} %all-gather.8.cloned.1.call-done), kind=kLoop, calls=%fused_computation.380 | loop fusion | bytes 7077888 | tf_op jit(solution)/shard_map/slice | solution.py:119
  265.6 14.4 %fusion.271 = (f32[12,256]{1,0:T(8,128)S(1)}, f32[12,256,2048]{2,1,0:T(8,128)}) fusion(pred[256,2048]{1,0:T(8,128)(4,1)} %broadcast_compare_fusion.1, bf16[256,12,64]{0,2,1:T(8,128)(2,1)S(1)} %bitcast.442, bf16[2048,12,64]{0,2,1:T(8,128)(2,1)} %bitcast.427), kind=kOutput, calls=%fused_computation.390 | convolution fusion | flops 830474240 | bytes 29241344 | tf_op jit(solution)/shard_map/sub | solution.py:51
  287.0 11.6 fusion.101
  300.7 7.4 convert_bitcast_fusion
  311.3 14.4 %fusion.269 = (f32[12,256]{1,0:T(8,128)S(1)}, f32[12,256,2048]{2,1,0:T(8,128)}) fusion(pred[256,2048]{1,0:T(8,128)(4,1)} %broadcast_compare_fusion, bf16[256,12,64]{0,2,1:T(8,128)(2,1)S(1)} %bitcast.444, bf16[2048,12,64]{0,2,1:T(8,128)(2,1)} %bitcast.429), kind=kOutput, calls=%fused_computation.388 | convolution fusion | flops 830474240 | bytes 29241344 | tf_op jit(solution)/shard_map/sub | solution.py:51
  325.8 11.5 fusion.104
  355.5 116.4 %reduce-scatter.15.cloned.1.call-done = f32[2048,96]{0,1:T(8,128)} async-done(((f32[2048,768]{0,1:T(8,128)}), f32[2048,96]{0,1:T(8,128)}) %reduce-scatter.15.cloned.1.call-update) | async-done | bytes 786448 | tf_op jit(solution)/shard_map/reduce_scatter | solution.py:289
  471.9 24.8 %reduce-scatter.17.cloned.1.call-done = f32[512,96]{0,1:T(8,128)} async-done(((f32[2048,96]{0,1:T(8,128)}), f32[512,96]{0,1:T(8,128)}) %reduce-scatter.17.cloned.1.call-update) | async-done | bytes 196624 | tf_op jit(solution)/shard_map/reduce_scatter | solution.py:295
  505.6 60.4 %all-gather.12.cloned.1.call-done = bf16[2048,768]{0,1:T(8,128)(2,1)} async-done(((bf16[2048,96]{0,1:T(8,128)(2,1)}), bf16[2048,768]{0,1:T(8,128)(2,1)}) %all-gather.12.cloned.1.call-update) | async-done | bytes 3145744 | tf_op jit(solution)/shard_map/all_gather | solution.py:265
  571.9 7.8 fusion.89
  591.4 11.2 fusion.29
  602.6 18.0 %multiply_reduce_fusion = (f32[12,256]{1,0:T(8,128)}, f32[12,256,2048]{2,1,0:T(8,128)}) fusion(f32[12,256,2048]{2,1,0:T(8,128)} %get-tuple-element.202, f32[12,256]{1,0:T(8,128)} %copy-done.110, bf16[256,12,64]{0,2,1:T(8,128)(2,1)} %bitcast.478, bf16[2048,12,64]{0,2,1:T(8,128)(2,1)} %bitcast.441), kind=kOutput, calls=%fused_computation.5 | convolution fusion | flops 824177664 | bytes 53895168 | tf_op jit(solution)/shard_map/qhe,khe->hqk/dot_general | solution.py:68
  621.4 11.8 add_bitcast_fusion
  633.9 12.0 fusion.26
  653.6 16.7 %multiply_convert_fusion = bf16[12,256,2048]{2,1,0:T(8,128)(2,1)S(1)} fusion(f32[12,256,2048]{2,1,0:T(8,128)} %get-tuple-element.215, f32[12,256]{1,0:T(8,128)} %get-tuple-element.214, f32[12,256,2048]{2,1,0:T(8,128)} %get-tuple-element.202, f32[12,256]{1,0:T(8,128)} %copy-done.110), kind=kLoop, calls=%fused_computation.4 | loop fusion | flops 25165824 | bytes 62939136 | tf_op jit(solution)/shard_map/convert_element_type | solution.py:75
  677.7 17.6 %multiply_reduce_fusion.1 = (f32[12,256]{1,0:T(8,128)S(1)}, f32[12,256,2048]{2,1,0:T(8,128)}) fusion(f32[12,256,2048]{2,1,0:T(8,128)} %get-tuple-element.208, f32[12,256]{1,0:T(8,128)S(1)} %copy-done.109, bf16[256,12,64]{0,2,1:T(8,128)(2,1)S(1)} %bitcast.472, bf16[2048,12,64]{0,2,1:T(8,128)(2,1)} %bitcast.439), kind=kOutput, calls=%fused_computation.7 | convolution fusion | flops 824177664 | bytes 53895168 | tf_op jit(solution)/shard_map/qhe,khe->hqk/dot_general | solution.py:68
  695.3 16.5 %multiply_convert_fusion.1 = bf16[12,256,2048]{2,1,0:T(8,128)(2,1)S(1)} fusion(f32[12,256,2048]{2,1,0:T(8,128)} %get-tuple-element.217, f32[12,256]{1,0:T(8,128)S(1)} %get-tuple-element.216, f32[12,256,2048]{2,1,0:T(8,128)} %get-tuple-element.208, f32[12,256]{1,0:T(8,128)S(1)} %copy-done.109), kind=kLoop, calls=%fused_computation.6 | loop fusion | flops 25165824 | bytes 62939136 | tf_op jit(solution)/shard_map/convert_element_type | solution.py:75
  719.9 9.8 fusion.99
  731.7 8.8 fusion.100
  784.2 7.4 bitcast_dynamic-update-slice_fusion.2
  801.4 8.9 bitcast_dynamic-update-slice_fusion.3
  812.3 13.1 %add.227 = f32[8,768,768]{1,2,0:T(8,128)} add(f32[8,768,768]{1,2,0:T(8,128)} %bitcast_dynamic-update-slice_fusion.7, f32[8,768,768]{1,2,0:T(8,128)S(1)} %bitcast_dynamic-update-slice_fusion.4) | non-fusion elementwise | flops 4718592 | bytes 56623104 | tf_op jit(solution)/shard_map/add | solution.py:357
  855.0 299.2 %reduce-scatter.11.cloned.1.call-done = f32[8,768,96]{1,2,0:T(8,128)} async-done(((f32[8,768,768]{1,2,0:T(8,128)}), f32[8,768,96]{1,2,0:T(8,128)}) %reduce-scatter.11.cloned.1.call-update) | async-done | bytes 2359312 | tf_op jit(solution)/shard_map/reduce_scatter | solution.py:287
  1184.6 9.1 maximum_bitcast_fusion
  1194.7 19.9 %psum.8 = f32[3,192]{1,0:T(4,128)S(1)} all-reduce(f32[3,192]{1,0:T(4,128)S(1)} %copy.478), channel_id=1, replica_groups=mesh['dp'=8,'fsdp'=4] {'dp'}, use_global_device_ids=true, to_apply=%region_36.37 | all-reduce | flops 576 | bytes 4608 | tf_op jit(solution)/shard_map/psum | solution.py:291
  1215.2 7.1 all-reduce.3.cloned.1.call-done
  1226.0 31.7 %reduce-scatter.19.cloned.1.call-done = f32[192,768]{1,0:T(8,128)} async-done(((f32[768,768]{1,0:T(8,128)}), f32[192,768]{1,0:T(8,128)}) %reduce-scatter.19.cloned.1.call-update) | async-done | bytes 589840
  (441 shorter events, 289.1 us)
Async XLA Ops:
  7.2 25.3 %all-gather.6.cloned.1.call-start = ((), (), s32[]{:S(2)}) async-start(), calls=%async_computation.6 | async-start | bytes 1966080 | tf_op jit(solution)/shard_map/all_gather | solution.py:257
  9.7 35.3 %copy-start.111 = (f32[3,192]{1,0:T(4,128)S(1)}, f32[3,192]{1,0:T(4,128)}, u32[]{:S(2)}) copy-start(f32[3,192]{1,0:T(4,128)} %param.31) | copy-start | bytes 6916
  9.7 35.3 %copy-start.127 = (s32[2,1,256]{2,1,0:T(1,128)S(1)}, s32[2,1,256]{2,1,0:T(1,128)}, u32[]{:S(2)}) copy-start(s32[2,1,256]{2,1,0:T(1,128)} %param.19) | copy-start | bytes 6148
  9.7 35.3 %copy-start.47 = (bf16[2,1,256,768]{3,2,1,0:T(8,128)(2,1)S(1)}, bf16[2,1,256,768]{3,2,1,0:T(8,128)(2,1)}, u32[]{:S(2)}) copy-start(bf16[2,1,256,768]{3,2,1,0:T(8,128)(2,1)} %param.17) | copy-start | bytes 2359300
  9.7 41.4 %copy-start.113 = (s32[2,1,2048]{2,1,0:T(1,128)S(1)}, s32[2,1,2048]{2,1,0:T(1,128)}, u32[]{:S(2)}) copy-start(s32[2,1,2048]{2,1,0:T(1,128)} %param.20) | copy-start | bytes 49156
  9.7 163.5 %all-gather.8.cloned.1.call-start = ((), (), s32[]{:S(2)}) async-start(), calls=%async_computation.7 | async-start | bytes 10616832 | tf_op jit(solution)/shard_map/all_gather | solution.py:263
  35.8 302.3 %all-gather.10.cloned.1.call-start = ((), (), s32[]{:S(2)}) async-start(), calls=%async_computation.8 | async-start | bytes 7077888 | tf_op jit(solution)/shard_map/all_gather | solution.py:264
  44.9 427.0 %reduce-scatter.15.cloned.1.call-start = ((), (), s32[]{:S(2)}) async-start(), calls=%async_computation.12 | async-start | bytes 7077888 | tf_op jit(solution)/shard_map/reduce_scatter | solution.py:289
  51.1 175.6 %copy-start.115 = (f32[768]{0:T(1024)}, f32[768]{0:T(1024)S(1)}, u32[]{:S(2)}) copy-start(f32[768]{0:T(1024)S(1)} %get-tuple-element.151) | copy-start | bytes 9220
  51.1 228.9 %copy-start.99 = (f32[768]{0:T(1024)}, f32[768]{0:T(1024)S(1)}, u32[]{:S(2)}) copy-start(f32[768]{0:T(1024)S(1)} %get-tuple-element.150) | copy-start | bytes 9220
  54.9 163.0 %copy-start.121 = (f32[256]{0:T(256)}, f32[256]{0:T(256)S(1)}, u32[]{:S(2)}) copy-start(f32[256]{0:T(256)S(1)} %get-tuple-element.225) | copy-start | bytes 3076
  54.9 171.8 %copy-start.123 = (f32[256]{0:T(256)}, f32[256]{0:T(256)S(1)}, u32[]{:S(2)}) copy-start(f32[256]{0:T(256)S(1)} %get-tuple-element.226) | copy-start | bytes 3076
  217.9 62.2 %copy-start.4 = (bf16[1,768,768]{2,1,0:T(8,128)(2,1)}, bf16[1,768,768]{2,1,0:T(8,128)(2,1)S(1)}, u32[]{:S(2)}) copy-start(bf16[1,768,768]{2,1,0:T(8,128)(2,1)S(1)} %copy.482) | copy-start | bytes 3538948
  241.7 56.9 %copy-start.8 = (f32[256,768]{1,0:T(8,128)}, f32[256,768]{1,0:T(8,128)S(1)}, u32[]{:S(2)}) copy-start(f32[256,768]{1,0:T(8,128)S(1)} %get-tuple-element.206) | copy-start | bytes 2359300
  249.7 87.6 %copy-start.10 = (f32[256,768]{1,0:T(8,128)}, f32[256,768]{1,0:T(8,128)S(1)}, u32[]{:S(2)}) copy-start(f32[256,768]{1,0:T(8,128)S(1)} %get-tuple-element.200) | copy-start | bytes 2359300
  249.8 30.2 %copy-start.103 = (f32[256]{0:T(256)}, f32[256]{0:T(256)S(1)}, u32[]{:S(2)}) copy-start(f32[256]{0:T(256)S(1)} %add_rsqrt_fusion.1) | copy-start | bytes 3076
  299.2 289.5 %copy-start.12 = (f32[256,768]{1,0:T(8,128)}, f32[256,768]{1,0:T(8,128)S(1)}, u32[]{:S(2)}) copy-start(f32[256,768]{1,0:T(8,128)S(1)} %get-tuple-element.210) | copy-start | bytes 2359300
  338.1 283.3 %copy-start.14 = (f32[256,768]{1,0:T(8,128)}, f32[256,768]{1,0:T(8,128)S(1)}, u32[]{:S(2)}) copy-start(f32[256,768]{1,0:T(8,128)S(1)} %get-tuple-element.212) | copy-start | bytes 2359300
  355.5 141.3 %reduce-scatter.17.cloned.1.call-start = ((), (), s32[]{:S(2)}) async-start(), calls=%async_computation.13 | async-start | bytes 983040 | tf_op jit(solution)/shard_map/reduce_scatter | solution.py:295
  471.9 94.1 %all-gather.12.cloned.1.call-start = ((), (), s32[]{:S(2)}) async-start(), calls=%async_computation.9 | async-start | bytes 3538944 | tf_op jit(solution)/shard_map/all_gather | solution.py:265
  505.5 333.9 %reduce-scatter.13.cloned.1.call-start = ((), (), s32[]{:S(2)}) async-start(), calls=%async_computation.11 | async-start | bytes 14155776 | tf_op jit(solution)/shard_map/reduce_scatter | solution.py:288
  633.2 521.0 %reduce-scatter.11.cloned.1.call-start = ((), (), s32[]{:S(2)}) async-start(), calls=%async_computation.10 | async-start | bytes 21233664 | tf_op jit(solution)/shard_map/reduce_scatter | solution.py:287
  825.4 368.3 %reduce-scatter.21.cloned.1.call-start = ((), (), s32[]{:S(2)}) async-start(), calls=%async_computation.15 | async-start | bytes 491520
  833.6 388.7 %all-reduce.3.cloned.1.call-start = ((), (), s32[]{:S(2)}) async-start(), calls=%async_computation.16 | async-start | bytes 3145728
  843.1 414.7 %reduce-scatter.19.cloned.1.call-start = ((), (), s32[]{:S(2)}) async-start(), calls=%async_computation.14 | async-start | bytes 2949120
  1184.6 30.0 %copy-start.112 = (f32[3,192]{1,0:T(4,128)S(1)}, f32[3,192]{1,0:T(4,128)}, u32[]{:S(2)}) copy-start(f32[3,192]{1,0:T(4,128)} %param.31) | copy-start | bytes 6916
  1184.6 30.0 %copy-start.117 = (f32[3,192]{1,0:T(4,128)S(1)}, f32[3,192]{1,0:T(4,128)}, u32[]{:S(2)}) copy-start(f32[3,192]{1,0:T(4,128)} %param.33) | copy-start | bytes 6916
  1184.6 30.0 %copy-start.118 = (f32[3,192]{1,0:T(4,128)S(1)}, f32[3,192]{1,0:T(4,128)}, u32[]{:S(2)}) copy-start(f32[3,192]{1,0:T(4,128)} %param.32) | copy-start | bytes 6916
  1184.6 38.9 %copy-start.76 = (f32[2,192,256]{2,1,0:T(8,128)S(1)}, f32[2,192,256]{2,1,0:T(8,128)}, u32[]{:S(2)}) copy-start(f32[2,192,256]{2,1,0:T(8,128)} %param.25) | copy-start | bytes 1179652
  1223.5 37.0 %copy-start.52 = (f32[8,192,96]{1,2,0:T(8,128)S(1)}, f32[8,192,96]{1,2,0:T(8,128)}, u32[]{:S(2)}) copy-start(f32[8,192,96]{1,2,0:T(8,128)} %copy.439) | copy-start | bytes 1769476
  1223.5 37.0 %copy-start.53 = (f32[8,192,96]{1,2,0:T(8,128)S(1)}, f32[8,192,96]{1,2,0:T(8,128)}, u32[]{:S(2)}) copy-start(f32[8,192,96]{1,2,0:T(8,128)} %copy.426) | copy-start | bytes 1769476
  1223.5 37.0 %copy-start.54 = (f32[8,192,96]{1,2,0:T(8,128)S(1)}, f32[8,192,96]{1,2,0:T(8,128)}, u32[]{:S(2)}) copy-start(f32[8,192,96]{1,2,0:T(8,128)} %copy.437) | copy-start | bytes 1769476
  (115 other events, 627.1 us)
Sparse Core Ops, SparseCore 0:
  10.1 22.3 all-gather.5
  35.9 137.2 all-gather.7
  175.2 97.6 all-gather.9
  355.6 116.2 reduce-scatter.14
  474.2 22.4 reduce-scatter.16
  505.7 60.2 all-gather.11
  633.3 206.0 reduce-scatter.12
  843.3 310.8 reduce-scatter.10
  1157.3 19.8 reduce-scatter.20
  1179.4 42.8 all-reduce.2
  1224.9 32.8 reduce-scatter.18
where the time goes:
time: 1280 us
  waiting for transfers between devices  686 us (54%)
  matrix products  296 us (23%)
  local copies, waits for them, and re-layouts  161 us (13%)
  other arithmetic  75.5 us (6%)
  blocking collectives  40.7 us (3%)
  between operations  16.7 us (1%)
    reduce_scatter x1, waiting for transfers between devices, reduce_grads(): lax.psum_scatter(totals[0], 'dp', scatter_dimension=2, tiled=True)  299 us
    all_gather x1, waiting for transfers between devices, fetch_forward(): lax.all_gather(widened[0], 'dp', axis=2, tiled=True)  118 us
    reduce_scatter x1, waiting for transfers between devices, reduce_grads(): lax.psum_scatter(totals[2], 'dp', scatter_dimension=1, tiled=True)  116 us
    unnamed x293, local copies, waits for them, and re-layouts  80.4 us
    all_gather x1, waiting for transfers between devices, fetch_forward(): lax.all_gather(widened[2], 'dp', axis=1, tiled=True)  60.4 us
    dot_general x4, matrix products, attend_backward(): jnp.einsum('qhe,khe->hqk', grad_mixture, value_heads, preferred_element_t...  41.4 us
    unnamed x14, waiting for transfers between devices  39 us
    sub x4, matrix products, softmax_rows(): raised = jnp.exp(scores - row_maximum)  37.1 us
  transfers between devices with their start and end apart: 11, of which 9 were waited for; matrix products, arithmetic and copies ran while one was open for 32% of the time, Pallas kernels for 0%

commit v1 on v0

--- a/solution.py
+++ b/solution.py
@@ -18,6 +18,19 @@
 rate_gain = 0.3
 float_type = jnp.float32
 brain_type = jnp.bfloat16
+
+
+def gather_around(array, axis, dim):
+    ways = lax.axis_size(axis)
+    up = [(d, (d + 1) % ways) for d in range(ways)]
+    down = [(d, (d - 1) % ways) for d in range(ways)]
+    earlier, later = ([array], [array])
+    for _ in range(ways // 2):
+        earlier.append(lax.ppermute(earlier[-1], axis, up))
+    for _ in range((ways - 1) // 2):
+        later.append(lax.ppermute(later[-1], axis, down))
+    line = jnp.concatenate([*earlier[::-1], *later[1:]], axis=dim)
+    return jnp.roll(line, (lax.axis_index(axis) - ways // 2) * array.shape[dim], axis=dim)
 
 
 def gelu_tanh(values):
@@ -260,7 +273,7 @@
         lax.all_gather(copies[3], "fsdp", axis=1, tiled=True),
     )
     complete = (
-        lax.all_gather(widened[0], "dp", axis=2, tiled=True),
+        gather_around(widened[0], "dp", 2),
         lax.all_gather(widened[1], "dp", axis=2, tiled=True),
         lax.all_gather(widened[2], "dp", axis=1, tiled=True),
     )

time: 1280 us -> 1390 us (1.086)
  waiting for transfers between devices: 686 us -> 760 us
  starting transfers between devices: 0.45 us -> 15.8 us
    ppermute x0 -> x7, waiting for transfers between devices: none -> 192 us  [the longest x4 192 us: gather_around(): earlier.append(lax.ppermute(earlier[-1], axis, up))]
    unnamed x14, waiting for transfers between devices: 39 us -> 0.19 us
    all_gather x1, waiting for transfers between devices: 60.4 us -> 23.6 us  [fetch_forward(): lax.all_gather(widened[2], 'dp', axis=1, tiled=True)]
    reduce_scatter x1, waiting for transfers between devices: 299 us -> 276 us  [reduce_grads(): lax.psum_scatter(totals[0], 'dp', scatter_dimension=2, tiled=True)]
    ppermute x0 -> x7, starting transfers between devices: none -> 14.9 us  [the longest x3 7.55 us: gather_around(): later.append(lax.ppermute(later[-1], axis, down))]
    unnamed x293 -> x301, local copies, waits for them, and re-layouts: 80.4 us -> 90.9 us
    slice x7 -> x3, local copies, waits for them, and re-layouts: 38.6 us -> 33.1 us  [the longest x1 18.4 us: layer_backward(): attention[3]]
  transfers between devices with their start and end apart: 11 -> 18, of which waited for: 9 -> 11; matrix products, arithmetic and copies ran while one was open for 32% -> 32% of each run, Pallas kernels for 0% -> 0%
where the time goes in v1:
time: 1390 us
  waiting for transfers between devices  760 us (55%)
  matrix products  301 us (22%)
  local copies, waits for them, and re-layouts  167 us (12%)
  other arithmetic  85 us (6%)
  blocking collectives  39.2 us (3%)
  between operations  18 us (1%)
  starting transfers between devices  15.8 us (1%)
    reduce_scatter x1, waiting for transfers between devices, reduce_grads(): lax.psum_scatter(totals[0], 'dp', scatter_dimension=2, tiled=True)  276 us
    ppermute x4, waiting for transfers between devices, gather_around(): earlier.append(lax.ppermute(earlier[-1], axis, up))  192 us
    reduce_scatter x1, waiting for transfers between devices, reduce_grads(): lax.psum_scatter(totals[2], 'dp', scatter_dimension=1, tiled=True)  117 us
    all_gather x1, waiting for transfers between devices, fetch_backward(): lax.all_gather(widened[0], 'dp', axis=2, tiled=True)  108 us
    unnamed x301, local copies, waits for them, and re-layouts  90.9 us
    dot_general x4, matrix products, attend_backward(): jnp.einsum('qhe,khe->hqk', grad_mixture, value_heads, preferred_element_t...  41.2 us
    sub x4, matrix products, softmax_rows(): raised = jnp.exp(scores - row_maximum)  34.7 us
    convert_element_type x4, other arithmetic, attend_backward(): grad_scores = (probabilities * (grad_probs - row_inner)).astype(brain_type)  34.4 us
  transfers between devices with their start and end apart: 18, of which 11 were waited for; matrix products, arithmetic and copies ran while one was open for 32% of the time, Pallas kernels for 0%

profile of v1, /device:TPU:0, one launch (start us, length us, event | category | flops | bytes accessed | tf_op | source)
XLA Modules:
  0.0 1386.8 jit_solution(3651425688531886120)
XLA Ops:
  10.6 22.8 %all-gather.6.cloned.1.call-done = bf16[8,768,96]{2,0,1:T(8,128)(2,1)} async-done(((bf16[8,192,96]{2,0,1:T(8,128)(2,1)}), bf16[8,768,96]{2,0,1:T(8,128)(2,1)}) %all-gather.6.cloned.1.call-update) | async-done | bytes 1179664 | tf_op jit(solution)/shard_map/all_gather | solution.py:270
  37.0 29.3 %collective-permute-done = bf16[8,768,96]{1,2,0:T(8,128)(2,1)S(1)} collective-permute-done((bf16[8,768,96]{1,2,0:T(8,128)(2,1)S(1)}, bf16[8,768,96]{1,2,0:T(8,128)(2,1)S(1)}, u32[]{:S(2)}, u32[]{:S(2)}) %collective-permute-start) | collective-permute-done | bytes 1179680 | tf_op jit(solution)/shard_map/ppermute | solution.py:29
  66.3 8.2 all_gather.16
  84.4 40.7 %collective-permute-done.1 = bf16[8,768,96]{1,2,0:T(8,128)(2,1)} collective-permute-done((bf16[8,768,96]{1,2,0:T(8,128)(2,1)S(1)}, bf16[8,768,96]{1,2,0:T(8,128)(2,1)}, u32[]{:S(2)}, u32[]{:S(2)}) %collective-permute-start.1) | collective-permute-done | bytes 1179680 | tf_op jit(solution)/shard_map/ppermute | solution.py:29
  132.2 61.7 %collective-permute-done.2 = bf16[8,768,96]{1,2,0:T(8,128)(2,1)} collective-permute-done((bf16[8,768,96]{1,2,0:T(8,128)(2,1)}, bf16[8,768,96]{1,2,0:T(8,128)(2,1)}, u32[]{:S(2)}, u32[]{:S(2)}) %collective-permute-start.2) | collective-permute-done | bytes 1179680 | tf_op jit(solution)/shard_map/ppermute | solution.py:29
  201.6 60.1 %collective-permute-done.3 = bf16[8,768,96]{1,2,0:T(8,128)(2,1)} collective-permute-done((bf16[8,768,96]{1,2,0:T(8,128)(2,1)}, bf16[8,768,96]{1,2,0:T(8,128)(2,1)}, u32[]{:S(2)}, u32[]{:S(2)}) %collective-permute-start.3) | collective-permute-done | bytes 1179680 | tf_op jit(solution)/shard_map/ppermute | solution.py:29
  268.8 10.8 fusion.12
  302.6 8.2 convert_bitcast_fusion.1
  314.1 14.4 %fusion.262 = (f32[12,256]{1,0:T(8,128)S(1)}, f32[12,256,2048]{2,1,0:T(8,128)}) fusion(pred[256,2048]{1,0:T(8,128)(4,1)S(1)} %copy-done.79, bf16[256,12,64]{0,2,1:T(8,128)(2,1)S(1)} %bitcast.446, bf16[2048,12,64]{0,2,1:T(8,128)(2,1)} %bitcast.431), kind=kOutput, calls=%fused_computation.394 | convolution fusion | flops 830474240 | bytes 29241344 | tf_op jit(solution)/shard_map/sub | solution.py:64
  330.5 11.7 fusion.98
  355.2 14.5 %fusion.260 = (f32[12,256]{1,0:T(8,128)S(1)}, f32[12,256,2048]{2,1,0:T(8,128)}) fusion(pred[256,2048]{1,0:T(8,128)(4,1)S(1)} %copy-done.78, bf16[256,12,64]{0,2,1:T(8,128)(2,1)S(1)} %bitcast.448, bf16[2048,12,64]{0,2,1:T(8,128)(2,1)} %bitcast.433), kind=kOutput, calls=%fused_computation.392 | convolution fusion | flops 830474240 | bytes 29241344 | tf_op jit(solution)/shard_map/sub | solution.py:64
  369.7 11.5 fusion.101
  401.0 116.7 %reduce-scatter.15.cloned.1.call-done = f32[2048,96]{0,1:T(8,128)} async-done(((f32[2048,768]{0,1:T(8,128)}), f32[2048,96]{0,1:T(8,128)}) %reduce-scatter.15.cloned.1.call-update) | async-done | bytes 786448 | tf_op jit(solution)/shard_map/reduce_scatter | solution.py:302
  519.9 20.5 %reduce-scatter.17.cloned.1.call-done = f32[512,96]{0,1:T(8,128)} async-done(((f32[2048,96]{0,1:T(8,128)}), f32[512,96]{0,1:T(8,128)}) %reduce-scatter.17.cloned.1.call-update) | async-done | bytes 196624 | tf_op jit(solution)/shard_map/reduce_scatter | solution.py:308
  549.0 108.4 %all-gather.12.cloned.1.call-done = bf16[8,768,768]{1,0,2:T(8,128)(2,1)} async-done(((bf16[8,768,96]{1,0,2:T(8,128)(2,1)}), bf16[8,768,768]{1,0,2:T(8,128)(2,1)}) %all-gather.12.cloned.1.call-update) | async-done | bytes 9437200 | tf_op jit(solution)/shard_map/all_gather | solution.py:291
  657.3 18.4 %fusion.252 = (bf16[1,768,768]{1,0,2:T(2,128)(2,1)}, bf16[1,768,768]{1,0,2:T(2,128)(2,1)}, bf16[1,768,768]{1,0,2:T(2,128)(2,1)}) fusion(bf16[8,768,768]{1,0,2:T(8,128)(2,1)} %all-gather.12.cloned.1.call-done), kind=kLoop, calls=%fused_computation.384 | loop fusion | bytes 7077888 | tf_op jit(solution)/shard_map/slice | solution.py:230
  694.1 23.6 %all-gather.10.cloned.1.call-done = bf16[2048,768]{0,1:T(8,128)(2,1)} async-done(((bf16[2048,96]{0,1:T(8,128)(2,1)}), bf16[2048,768]{0,1:T(8,128)(2,1)}) %all-gather.10.cloned.1.call-update) | async-done | bytes 3145744 | tf_op jit(solution)/shard_map/all_gather | solution.py:278
  742.0 11.7 fusion.30
  753.8 17.5 %multiply_reduce_fusion = (f32[12,256]{1,0:T(8,128)}, f32[12,256,2048]{2,1,0:T(8,128)}) fusion(f32[12,256,2048]{2,1,0:T(8,128)} %get-tuple-element.203, f32[12,256]{1,0:T(8,128)S(1)} %copy-done.110, bf16[256,12,64]{0,2,1:T(8,128)(2,1)S(1)} %bitcast.482, bf16[2048,12,64]{0,2,1:T(8,128)(2,1)} %bitcast.445), kind=kOutput, calls=%fused_computation.5 | convolution fusion | flops 824177664 | bytes 53895168 | tf_op jit(solution)/shard_map/qhe,khe->hqk/dot_general | solution.py:81
  772.0 11.8 add_bitcast_fusion
  784.5 12.0 fusion.27
  804.2 16.7 %multiply_convert_fusion = bf16[12,256,2048]{2,1,0:T(8,128)(2,1)S(1)} fusion(f32[12,256,2048]{2,1,0:T(8,128)} %get-tuple-element.216, f32[12,256]{1,0:T(8,128)} %get-tuple-element.215, f32[12,256,2048]{2,1,0:T(8,128)} %get-tuple-element.203, f32[12,256]{1,0:T(8,128)} %copy-done.109), kind=kLoop, calls=%fused_computation.4 | loop fusion | flops 25165824 | bytes 62939136 | tf_op jit(solution)/shard_map/convert_element_type | solution.py:88
  828.2 17.7 %multiply_reduce_fusion.1 = (f32[12,256]{1,0:T(8,128)S(1)}, f32[12,256,2048]{2,1,0:T(8,128)}) fusion(f32[12,256,2048]{2,1,0:T(8,128)} %get-tuple-element.209, f32[12,256]{1,0:T(8,128)S(1)} %copy-done.108, bf16[256,12,64]{0,2,1:T(8,128)(2,1)S(1)} %bitcast.476, bf16[2048,12,64]{0,2,1:T(8,128)(2,1)} %bitcast.443), kind=kOutput, calls=%fused_computation.7 | convolution fusion | flops 824177664 | bytes 53895168 | tf_op jit(solution)/shard_map/qhe,khe->hqk/dot_general | solution.py:81
  846.0 16.5 %multiply_convert_fusion.1 = bf16[12,256,2048]{2,1,0:T(8,128)(2,1)S(1)} fusion(f32[12,256,2048]{2,1,0:T(8,128)} %get-tuple-element.218, f32[12,256]{1,0:T(8,128)S(1)} %get-tuple-element.217, f32[12,256,2048]{2,1,0:T(8,128)} %get-tuple-element.209, f32[12,256]{1,0:T(8,128)S(1)} %copy-done.108), kind=kLoop, calls=%fused_computation.6 | loop fusion | flops 25165824 | bytes 62939136 | tf_op jit(solution)/shard_map/convert_element_type | solution.py:88
  870.5 9.8 fusion.96
  882.2 8.8 fusion.97
  950.0 8.9 bitcast_dynamic-update-slice_fusion.3
  960.8 13.0 add.236
  981.0 8.1 copy.445
  1026.6 275.9 %reduce-scatter.11.cloned.1.call-done = f32[8,768,96]{1,2,0:T(8,128)} async-done(((f32[8,768,768]{1,2,0:T(8,128)}), f32[8,768,96]{1,2,0:T(8,128)}) %reduce-scatter.11.cloned.1.call-update) | async-done | bytes 2359312 | tf_op jit(solution)/shard_map/reduce_scatter | solution.py:300
  1332.9 9.6 maximum_bitcast_fusion
  1343.5 19.3 %psum.8 = f32[3,192]{1,0:T(4,128)S(1)} all-reduce(f32[3,192]{1,0:T(4,128)S(1)} %copy.441), channel_id=1, replica_groups=mesh['dp'=8,'fsdp'=4] {'dp'}, use_global_device_ids=true, to_apply=%region_36.38 | all-reduce | flops 576 | bytes 4608 | tf_op jit(solution)/shard_map/psum | solution.py:304
  (459 shorter events, 330.1 us)
Async XLA Ops:
  8.0 58.3 %copy-start.69 = (f32[2,192,256]{2,1,0:T(8,128)S(1)}, f32[2,192,256]{2,1,0:T(8,128)}, u32[]{:S(2)}) copy-start(f32[2,192,256]{2,1,0:T(8,128)} %param.27) | copy-start | bytes 1179652
  8.0 71.1 %copy-start.111 = (f32[3,192]{1,0:T(4,128)S(1)}, f32[3,192]{1,0:T(4,128)}, u32[]{:S(2)}) copy-start(f32[3,192]{1,0:T(4,128)} %param.33) | copy-start | bytes 6916
  8.0 119.6 %copy-start.131 = (s32[2,1,256]{2,1,0:T(1,128)S(1)}, s32[2,1,256]{2,1,0:T(1,128)}, u32[]{:S(2)}) copy-start(s32[2,1,256]{2,1,0:T(1,128)} %param.21) | copy-start | bytes 6148
  8.1 25.3 %all-gather.6.cloned.1.call-start = ((), (), s32[]{:S(2)}) async-start(), calls=%async_computation.6 | async-start | bytes 1966080 | tf_op jit(solution)/shard_map/all_gather | solution.py:270
  10.5 121.5 %copy-start.44 = (bf16[2,1,256,768]{3,2,1,0:T(8,128)(2,1)S(1)}, bf16[2,1,256,768]{3,2,1,0:T(8,128)(2,1)}, u32[]{:S(2)}) copy-start(bf16[2,1,256,768]{3,2,1,0:T(8,128)(2,1)} %param.19) | copy-start | bytes 2359300
  10.5 372.9 %all-gather.8.cloned.1.call-start = ((), (), s32[]{:S(2)}) async-start(), calls=%async_computation.7 | async-start | bytes 7077888 | tf_op jit(solution)/shard_map/all_gather | solution.py:277
  35.4 30.8 %collective-permute-start = (bf16[8,768,96]{1,2,0:T(8,128)(2,1)S(1)}, bf16[8,768,96]{1,2,0:T(8,128)(2,1)S(1)}, u32[]{:S(2)}, u32[]{:S(2)}) collective-permute-start(bf16[8,768,96]{1,2,0:T(8,128)(2,1)S(1)} %copy.357), channel_id=1, source_target_pairs={{0,4},{4,8},{8,12},{12,16},{16,20},{20,24},{24,28},{28,0},{1,5},{5... | collective-permute-start | bytes 3538952 | tf_op jit(solution)/shard_map/ppermute | solution.py:29
  66.3 58.8 %collective-permute-start.1 = (bf16[8,768,96]{1,2,0:T(8,128)(2,1)S(1)}, bf16[8,768,96]{1,2,0:T(8,128)(2,1)}, u32[]{:S(2)}, u32[]{:S(2)}) collective-permute-start(bf16[8,768,96]{1,2,0:T(8,128)(2,1)S(1)} %collective-permute-done), channel_id=1, source_target_pairs={{0,4},{4,8},{8,12},{12,16},{16,20},{20,24},{24,28},{28,0},{1,5},{5... | collective-permute-start | bytes 3538952 | tf_op jit(solution)/shard_map/ppermute | solution.py:29
  74.5 443.1 %reduce-scatter.15.cloned.1.call-start = ((), (), s32[]{:S(2)}) async-start(), calls=%async_computation.12 | async-start | bytes 7077888 | tf_op jit(solution)/shard_map/reduce_scatter | solution.py:302
  74.6 55.8 %collective-permute-start.4 = (bf16[8,768,96]{1,2,0:T(8,128)(2,1)S(1)}, bf16[8,768,96]{1,2,0:T(8,128)(2,1)}, u32[]{:S(2)}, u32[]{:S(2)}) collective-permute-start(bf16[8,768,96]{1,2,0:T(8,128)(2,1)S(1)} %copy.357), channel_id=1, source_target_pairs={{0,28},{4,0},{8,4},{12,8},{16,12},{20,16},{24,20},{28,24},{1,29},{... | collective-permute-start | bytes 3538952 | tf_op jit(solution)/shard_map/ppermute | solution.py:31
  125.0 68.9 %collective-permute-start.2 = (bf16[8,768,96]{1,2,0:T(8,128)(2,1)}, bf16[8,768,96]{1,2,0:T(8,128)(2,1)}, u32[]{:S(2)}, u32[]{:S(2)}) collective-permute-start(bf16[8,768,96]{1,2,0:T(8,128)(2,1)} %collective-permute-done.1), channel_id=1, source_target_pairs={{0,4},{4,8},{8,12},{12,16},{16,20},{20,24},{24,28},{28,0},{1,5},{5... | collective-permute-start | bytes 3538952 | tf_op jit(solution)/shard_map/ppermute | solution.py:29
  130.4 69.7 %collective-permute-start.5 = (bf16[8,768,96]{1,2,0:T(8,128)(2,1)}, bf16[8,768,96]{1,2,0:T(8,128)(2,1)}, u32[]{:S(2)}, u32[]{:S(2)}) collective-permute-start(bf16[8,768,96]{1,2,0:T(8,128)(2,1)} %collective-permute-done.4), channel_id=1, source_target_pairs={{0,28},{4,0},{8,4},{12,8},{16,12},{20,16},{24,20},{28,24},{1,29},{... | collective-permute-start | bytes 3538952 | tf_op jit(solution)/shard_map/ppermute | solution.py:31
  193.9 67.7 %collective-permute-start.3 = (bf16[8,768,96]{1,2,0:T(8,128)(2,1)}, bf16[8,768,96]{1,2,0:T(8,128)(2,1)}, u32[]{:S(2)}, u32[]{:S(2)}) collective-permute-start(bf16[8,768,96]{1,2,0:T(8,128)(2,1)} %collective-permute-done.2), channel_id=1, source_target_pairs={{0,4},{4,8},{8,12},{12,16},{16,20},{20,24},{24,28},{28,0},{1,5},{5... | collective-permute-start | bytes 3538952 | tf_op jit(solution)/shard_map/ppermute | solution.py:29
  197.8 84.7 %copy-start.113 = (f32[768]{0:T(1024)}, f32[768]{0:T(1024)S(1)}, u32[]{:S(2)}) copy-start(f32[768]{0:T(1024)S(1)} %get-tuple-element.152) | copy-start | bytes 9220
  197.8 130.7 %copy-start.100 = (f32[768]{0:T(1024)}, f32[768]{0:T(1024)S(1)}, u32[]{:S(2)}) copy-start(f32[768]{0:T(1024)S(1)} %get-tuple-element.151) | copy-start | bytes 9220
  200.1 68.6 %collective-permute-start.6 = (bf16[8,768,96]{1,2,0:T(8,128)(2,1)}, bf16[8,768,96]{1,2,0:T(8,128)(2,1)S(1)}, u32[]{:S(2)}, u32[]{:S(2)}) collective-permute-start(bf16[8,768,96]{1,2,0:T(8,128)(2,1)} %collective-permute-done.5), channel_id=1, source_target_pairs={{0,28},{4,0},{8,4},{12,8},{16,12},{20,16},{24,20},{28,24},{1,29},{... | collective-permute-start | bytes 3538952 | tf_op jit(solution)/shard_map/ppermute | solution.py:31
  201.6 78.1 %copy-start.127 = (f32[256]{0:T(256)}, f32[256]{0:T(256)S(1)}, u32[]{:S(2)}) copy-start(f32[256]{0:T(256)S(1)} %get-tuple-element.227) | copy-start | bytes 3076
  201.6 80.9 %copy-start.124 = (f32[256]{0:T(256)}, f32[256]{0:T(256)S(1)}, u32[]{:S(2)}) copy-start(f32[256]{0:T(256)S(1)} %get-tuple-element.226) | copy-start | bytes 3076
  293.0 88.3 %copy-start.16 = (f32[256,768]{1,0:T(8,128)}, f32[256,768]{1,0:T(8,128)S(1)}, u32[]{:S(2)}) copy-start(f32[256,768]{1,0:T(8,128)S(1)} %get-tuple-element.201) | copy-start | bytes 2359300
  344.2 395.8 %copy-start.6 = (f32[256,768]{1,0:T(8,128)}, f32[256,768]{1,0:T(8,128)S(1)}, u32[]{:S(2)}) copy-start(f32[256,768]{1,0:T(8,128)S(1)} %get-tuple-element.211) | copy-start | bytes 2359300
  383.3 388.7 %copy-start.8 = (f32[256,768]{1,0:T(8,128)}, f32[256,768]{1,0:T(8,128)S(1)}, u32[]{:S(2)}) copy-start(f32[256,768]{1,0:T(8,128)S(1)} %get-tuple-element.213) | copy-start | bytes 2359300
  400.5 117.2 %copy-start.27 = (bf16[8,768,96]{2,0,1:T(8,128)(2,1)S(1)}, bf16[8,768,96]{2,0,1:T(8,128)(2,1)}, u32[]{:S(2)}) copy-start(bf16[8,768,96]{2,0,1:T(8,128)(2,1)} %all-gather.6.cloned.1.call-done) | copy-start | bytes 3538948
  400.5 139.9 %copy-start.98 = (f32[512,96]{0,1:T(8,128)S(1)}, f32[512,96]{0,1:T(8,128)}, u32[]{:S(2)}) copy-start(f32[512,96]{0,1:T(8,128)} %param.30) | copy-start | bytes 589828
  400.5 139.9 %copy-start.99 = (f32[512,96]{0,1:T(8,128)S(1)}, f32[512,96]{0,1:T(8,128)}, u32[]{:S(2)}) copy-start(f32[512,96]{0,1:T(8,128)} %param.32) | copy-start | bytes 589828
  400.5 139.8 %reduce-scatter.17.cloned.1.call-start = ((), (), s32[]{:S(2)}) async-start(), calls=%async_computation.13 | async-start | bytes 983040 | tf_op jit(solution)/shard_map/reduce_scatter | solution.py:308
  517.7 139.7 %all-gather.12.cloned.1.call-start = ((), (), s32[]{:S(2)}) async-start(), calls=%async_computation.9 | async-start | bytes 10616832 | tf_op jit(solution)/shard_map/all_gather | solution.py:291
  519.9 197.9 %all-gather.10.cloned.1.call-start = ((), (), s32[]{:S(2)}) async-start(), calls=%async_computation.8 | async-start | bytes 3538944 | tf_op jit(solution)/shard_map/all_gather | solution.py:278
  548.9 448.2 %reduce-scatter.13.cloned.1.call-start = ((), (), s32[]{:S(2)}) async-start(), calls=%async_computation.11 | async-start | bytes 14155776 | tf_op jit(solution)/shard_map/reduce_scatter | solution.py:301
  783.8 518.6 %reduce-scatter.11.cloned.1.call-start = ((), (), s32[]{:S(2)}) async-start(), calls=%async_computation.10 | async-start | bytes 21233664 | tf_op jit(solution)/shard_map/reduce_scatter | solution.py:300
  973.9 368.7 %reduce-scatter.21.cloned.1.call-start = ((), (), s32[]{:S(2)}) async-start(), calls=%async_computation.15 | async-start | bytes 491520
  997.0 366.4 %all-reduce.3.cloned.1.call-start = ((), (), s32[]{:S(2)}) async-start(), calls=%async_computation.16 | async-start | bytes 3145728
  1000.9 366.3 %reduce-scatter.19.cloned.1.call-start = ((), (), s32[]{:S(2)}) async-start(), calls=%async_computation.14 | async-start | bytes 2949120
  (122 other events, 821.6 us)
Sparse Core Ops, SparseCore 0:
  11.0 22.3 all-gather.5
  517.8 22.5 reduce-scatter.16
  1001.0 42.0 all-reduce.2
Sparse Core Ops, SparseCore 1:
  74.6 203.6 all-gather.7
  400.6 117.0 reduce-scatter.14
  520.9 136.4 all-gather.11
  659.6 58.1 all-gather.9
  783.9 205.9 reduce-scatter.12
  993.8 308.6 reduce-scatter.10
  1305.4 19.8 reduce-scatter.20
  1327.7 32.7 reduce-scatter.18
